TPU v7x, 32 devices: a whole 2x2x4 slice. The times are simulated.
32 devices in a mesh: rep: 2 (over x), dp: 16 (over y, z, core).
Axes of the slice: x: 2, y: 2, z: 4, core: 2. Of those that a mesh axis runs over, the one named last changes fastest.
Arguments:
- g_w_gate: bfloat16 [32, 2, 1280, 4096], P(('rep', 'dp')), parts along dimension 0
- g_w_up: bfloat16 [32, 2, 1280, 4096], P(('rep', 'dp')), parts along dimension 0
- g_w_down: bfloat16 [32, 2, 4096, 1280], P(('rep', 'dp')), parts along dimension 0
- w_gate: bfloat16 [2, 1280, 4096], replicated
- w_up: bfloat16 [2, 1280, 4096], replicated
- w_down: bfloat16 [2, 4096, 1280], replicated
- m_w_gate: float32 [2, 1280, 4096], P(None, 'dp')
- m_w_up: float32 [2, 1280, 4096], P(None, 'dp')
- m_w_down: float32 [2, 4096, 1280], P(None, 'dp')
- v_w_gate: float32 [2, 1280, 4096], P(None, 'dp')
- v_w_up: float32 [2, 1280, 4096], P(None, 'dp')
- v_w_down: float32 [2, 4096, 1280], P(None, 'dp')
Outputs:
- output 1: bfloat16 [4, 1280, 4096], P('rep'), parts along dimension 0
- output 2: bfloat16 [4, 1280, 4096], P('rep'), parts along dimension 0
- output 3: bfloat16 [4, 4096, 1280], P('rep'), parts along dimension 0
- output 4: float32 [4, 1280, 4096], P('rep', 'dp'), parts along dimension 0
- output 5: float32 [4, 1280, 4096], P('rep', 'dp'), parts along dimension 0
- output 6: float32 [4, 4096, 1280], P('rep', 'dp'), parts along dimension 0
- output 7: float32 [4, 1280, 4096], P('rep', 'dp'), parts along dimension 0
- output 8: float32 [4, 1280, 4096], P('rep', 'dp'), parts along dimension 0
- output 9: float32 [4, 4096, 1280], P('rep', 'dp'), parts along dimension 0
There are 2 independent parts. A program takes and returns all parts, laid end to end along the dimension named above; an argument that names none is the same for every part.
All inputs are finite; a program needn't handle non-finite values.
Results may differ from a plain program's by a relative error of at most 0.022.
Values are sent between devices in bfloat16 or wider.
A program may use at most 2 GiB of HBM per device.

v0:
```python
import jax
import jax.numpy as jnp
from jax import lax
from jax.sharding import PartitionSpec as P


def adamw(w, m, v, g):
    m = 0.9 * m + 0.1 * g
    v = 0.95 * v + 0.05 * g * g
    step = m * lax.rsqrt(v + 1e-8) + 0.1 * w
    return (w - 0.02 * step).astype(jnp.bfloat16), m, v


def solution(mesh):
    def step(*arrays):
        terms, weights, m, v = (arrays[i : i + 3] for i in (0, 3, 6, 9))
        gradients = [lax.psum_scatter(t[0], "dp", scatter_dimension=1, tiled=True).astype(jnp.float32) for t in terms]
        me = lax.axis_index("dp")
        own = [lax.dynamic_slice_in_dim(w, me * one.shape[1], one.shape[1], 1).astype(jnp.float32) for w, one in zip(weights, m, strict=True)]
        new = [adamw(w, m, v, g) for w, m, v, g in zip(own, m, v, gradients, strict=True)]
        whole = [lax.all_gather(one[0], "dp", axis=1, tiled=True) for one in new]
        return (*whole, *(one[1] for one in new), *(one[2] for one in new))

    all_of, cut = P(None, None, None), P(None, "dp", None)
    return jax.shard_map(
        step,
        mesh=mesh,
        in_specs=(P(("rep", "dp"), None, None, None),) * 3 + (all_of,) * 3 + (cut,) * 6,
        out_specs=(P("rep", None, None),) * 3 + (P("rep", "dp", None),) * 6,
        check_vma=False,
    )
```

profile of v0, /device:TPU:0, one launch (start us, length us, event | category | flops | bytes accessed | tf_op | source)
XLA Modules:
  0.0 1026.3 jit_solution(10831868185919416514)
XLA Ops:
  7.2 0.0 reduce-scatter.8.cloned.1.call-start
  7.2 0.7 reduce-scatter.8.cloned.1.call-update
  7.9 0.0 reduce-scatter.6.cloned.1.call-start
  8.0 0.7 reduce-scatter.6.cloned.1.call-update
  8.7 0.0 reduce-scatter.4.cloned.1.call-start
  8.7 0.0 copy-start.1
  8.7 0.7 reduce-scatter.4.cloned.1.call-update
  9.4 0.0 all-gather.8.cloned.1.call-start
  9.4 213.5 %reduce-scatter.8.cloned.1.call-done = bf16[2,256,1280]{2,1,0:T(8,128)(2,1)} async-done(((bf16[2,4096,1280]{2,1,0:T(8,128)(2,1)}), bf16[2,256,1280]{2,1,0:T(8,128)(2,1)}) %reduce-scatter.8.cloned.1.call-update) | async-done | bytes 1310736 | tf_op jit(solution)/shard_map/reduce_scatter | solution.py:17
  223.0 0.0 copy-done.1
  223.0 6.0 fusion.10
  229.0 0.0 all-gather.8.cloned.1.call-update
  229.1 0.0 all-gather.6.cloned.1.call-start
  229.1 205.4 %reduce-scatter.6.cloned.1.call-done = bf16[2,80,4096]{2,1,0:T(8,128)(2,1)} async-done(((bf16[2,1280,4096]{2,1,0:T(8,128)(2,1)}), bf16[2,80,4096]{2,1,0:T(8,128)(2,1)}) %reduce-scatter.6.cloned.1.call-update) | async-done | bytes 1310736 | tf_op jit(solution)/shard_map/reduce_scatter | solution.py:17
  434.5 0.0 copy-start.2
  434.5 7.0 fusion.6
  441.5 0.0 all-gather.6.cloned.1.call-update
  441.5 0.0 all-gather.4.cloned.1.call-start
  441.6 204.4 %reduce-scatter.4.cloned.1.call-done = bf16[2,80,4096]{2,1,0:T(8,128)(2,1)} async-done(((bf16[2,1280,4096]{2,1,0:T(8,128)(2,1)}), bf16[2,80,4096]{2,1,0:T(8,128)(2,1)}) %reduce-scatter.4.cloned.1.call-update) | async-done | bytes 1310736 | tf_op jit(solution)/shard_map/reduce_scatter | solution.py:17
  646.0 0.0 copy-done.2
  646.0 6.0 fusion.2
  652.1 0.0 all-gather.4.cloned.1.call-update
  652.1 103.9 %all-gather.8.cloned.1.call-done = bf16[2,4096,1280]{2,1,0:T(8,128)(2,1)} async-done(((bf16[2,256,1280]{2,1,0:T(8,128)(2,1)}), bf16[2,4096,1280]{2,1,0:T(8,128)(2,1)}) %all-gather.8.cloned.1.call-update) | async-done | bytes 20971536 | tf_op jit(solution)/shard_map/all_gather | solution.py:21
  756.0 110.7 %all-gather.6.cloned.1.call-done = bf16[2,1280,4096]{2,1,0:T(8,128)(2,1)} async-done(((bf16[2,80,4096]{2,1,0:T(8,128)(2,1)}), bf16[2,1280,4096]{2,1,0:T(8,128)(2,1)}) %all-gather.6.cloned.1.call-update) | async-done | bytes 20971536 | tf_op jit(solution)/shard_map/all_gather | solution.py:21
  866.7 110.7 %all-gather.4.cloned.1.call-done = bf16[2,1280,4096]{2,1,0:T(8,128)(2,1)} async-done(((bf16[2,80,4096]{2,1,0:T(8,128)(2,1)}), bf16[2,1280,4096]{2,1,0:T(8,128)(2,1)}) %all-gather.4.cloned.1.call-update) | async-done | bytes 20971536 | tf_op jit(solution)/shard_map/all_gather | solution.py:21
  977.3 0.0 copy-start
  977.3 0.0 slice-start
  977.3 0.0 slice-start.1
  977.3 0.0 slice-start.2
  977.3 21.1 %copy.24 = bf16[2,1280,4096]{2,1,0:T(8,128)(2,1)} copy(bf16[2,1280,4096]{2,1,0:T(8,128)(2,1)} %all-gather.4.cloned.1.call-done) | data formatting | bytes 41943040
  998.5 0.0 copy-done
  998.5 0.0 slice-start.3
  998.5 0.0 slice-start.4
  998.5 10.6 %copy.25 = bf16[2,1280,4096]{2,1,0:T(8,128)(2,1)} copy(bf16[2,1280,4096]{2,1,0:T(8,128)(2,1)S(1)} %copy-done) | data formatting | bytes 41943040
  1009.1 0.0 slice-done
  1009.1 0.0 slice-done.1
  1009.1 0.0 slice-done.2
  1009.1 1.6 slice-done.3
  1010.7 1.2 slice-done.4
  1011.9 7.5 copy.26
  (1 shorter events, 0.0 us)
Async XLA Ops:
  7.2 215.8 %reduce-scatter.8.cloned.1.call-start = ((), (), s32[]{:S(2)}) async-start(), calls=%async_computation.7 | async-start | bytes 22282240 | tf_op jit(solution)/shard_map/reduce_scatter | solution.py:17
  7.9 426.6 %reduce-scatter.6.cloned.1.call-start = ((), (), s32[]{:S(2)}) async-start(), calls=%async_computation.5 | async-start | bytes 22282240 | tf_op jit(solution)/shard_map/reduce_scatter | solution.py:17
  8.7 637.3 %reduce-scatter.4.cloned.1.call-start = ((), (), s32[]{:S(2)}) async-start(), calls=%async_computation.3 | async-start | bytes 22282240 | tf_op jit(solution)/shard_map/reduce_scatter | solution.py:17
  8.7 214.3 %copy-start.1 = (f32[2,256,1280]{2,1,0:T(8,128)S(1)}, f32[2,256,1280]{2,1,0:T(8,128)}, u32[]{:S(2)}) copy-start(f32[2,256,1280]{2,1,0:T(8,128)} %param.23) | copy-start | bytes 7864324
  9.4 746.6 %all-gather.8.cloned.1.call-start = ((), (), s32[]{:S(2)}) async-start(), calls=%async_computation.8 | async-start | bytes 22282240 | tf_op jit(solution)/shard_map/all_gather | solution.py:21
  229.1 637.6 %all-gather.6.cloned.1.call-start = ((), (), s32[]{:S(2)}) async-start(), calls=%async_computation.6 | async-start | bytes 22282240 | tf_op jit(solution)/shard_map/all_gather | solution.py:21
  434.5 211.5 %copy-start.2 = (f32[2,80,4096]{2,1,0:T(8,128)S(1)}, f32[2,80,4096]{2,1,0:T(8,128)}, u32[]{:S(2)}) copy-start(f32[2,80,4096]{2,1,0:T(8,128)} %param.21) | copy-start | bytes 7864324
  441.5 535.8 %all-gather.4.cloned.1.call-start = ((), (), s32[]{:S(2)}) async-start(), calls=%async_computation.4 | async-start | bytes 22282240 | tf_op jit(solution)/shard_map/all_gather | solution.py:21
  977.3 21.1 %copy-start = (bf16[2,1280,4096]{2,1,0:T(8,128)(2,1)S(1)}, bf16[2,1280,4096]{2,1,0:T(8,128)(2,1)}, u32[]{:S(2)}) copy-start(bf16[2,1280,4096]{2,1,0:T(8,128)(2,1)} %all-gather.6.cloned.1.call-done) | copy-start | bytes 62914564
  977.3 31.7 %slice-start = ((s8[20971520]{0:T(1024)(128)(4,1)}), s8[4194304]{0:T(1024)(128)(4,1)S(1)}, s32[]{:S(2)}) async-start(s8[20971520]{0:T(1024)(128)(4,1)} %bitcast.6), calls=%async_computation.9 | async-start | bytes 8388608
  977.3 31.7 %slice-start.1 = ((s8[20971520]{0:T(1024)(128)(4,1)}), s8[4194304]{0:T(1024)(128)(4,1)S(1)}, s32[]{:S(2)}) async-start(s8[20971520]{0:T(1024)(128)(4,1)} %bitcast.6), calls=%async_computation.10 | async-start | bytes 8388608
  977.3 31.7 %slice-start.2 = ((s8[20971520]{0:T(1024)(128)(4,1)}), s8[4194304]{0:T(1024)(128)(4,1)S(1)}, s32[]{:S(2)}) async-start(s8[20971520]{0:T(1024)(128)(4,1)} %bitcast.6), calls=%async_computation.11 | async-start | bytes 8388608
  998.5 12.3 %slice-start.3 = ((s8[20971520]{0:T(1024)(128)(4,1)}), s8[4194304]{0:T(1024)(128)(4,1)S(1)}, s32[]{:S(2)}) async-start(s8[20971520]{0:T(1024)(128)(4,1)} %bitcast.6), calls=%async_computation.12 | async-start | bytes 8388608
  998.5 13.4 %slice-start.4 = ((s8[20971520]{0:T(1024)(128)(4,1)}), s8[4194304]{0:T(1024)(128)(4,1)S(1)}, s32[]{:S(2)}) async-start(s8[20971520]{0:T(1024)(128)(4,1)} %bitcast.6), calls=%async_computation.13 | async-start | bytes 8388608
Sparse Core Ops, SparseCore 0:
  12.1 210.8 reduce-scatter.7
  227.1 207.3 reduce-scatter.5
  438.6 207.3 reduce-scatter.3
  648.0 107.9 all-gather.7
  758.0 108.6 all-gather.5
  868.6 108.6 all-gather.3
where the time goes:
time: 1030 us
  waiting for transfers between devices  951 us (92%)
  local copies, waits for them, and re-layouts  42.1 us (4%)
  other arithmetic  19.1 us (2%)
  between operations  14.1 us (1%)
    reduce_scatter x3, waiting for transfers between devices, step(): lax.psum_scatter(t[0], 'dp', scatter_dimension=1, tiled=True)  623 us
    all_gather x3, waiting for transfers between devices, step(): whole = [lax.all_gather(one[0], 'dp', axis=1, tiled=True) for one in new]  325 us
    unnamed x19, local copies, waits for them, and re-layouts  42.1 us
  transfers between devices with their start and end apart: 6, of which 6 were waited for; matrix products, arithmetic and copies ran while one was open for 2% of the time, Pallas kernels for 0%

commit v1 on v0

v1 whole, which is shorter than its diff:
```python
import functools

import jax
import jax.numpy as jnp
from jax import lax
from jax.experimental import pallas as pl
from jax.experimental.pallas import tpu as pltpu
from jax.sharding import PartitionSpec as P

MESH = pl.DeviceIdType.MESH
F32, BF16 = jnp.float32, jnp.bfloat16
Y, Z, C = 2, 4, 2
SPLIT = 16
RING = 8
SENDS = 4
DRAIN = 2
LAST = 10 + DRAIN


def kernel(split, tiles, *refs):
    g, w, m, v = (refs[i : i + 3] for i in (0, 3, 6, 9))
    out, moments = refs[12:14]
    (own_a, part_a, y_a, l_a, r_a, sy_a, sl_a, sr_a, own_b, part_b, y_b, l_b, r_b, sy_b, sl_b, sr_b) = refs[14:30]
    (w_a, m_a, v_a, w_b, m_b, v_b, nw_a, nm_a, nv_a, nw_b, nm_b, nv_b) = refs[30:42]
    local_sem, send_sem, recv_sem = refs[42:45]

    me = lax.axis_index("dp")
    c, z, y = lax.rem(me, C), lax.rem(lax.div(me, C), Z), lax.div(me, C * Z)
    other_c, other_y = 1 - c, 1 - y
    mate = {"dp": me + 1 - 2 * c}
    across = {"dp": me + (1 - 2 * y) * (Z * C)}
    right, left = {"dp": me + C}, {"dp": me - C}
    n = 6 * split
    big, small = 3 * tiles // 5 // split, 2 * tiles // 5 // split

    barrier = pltpu.get_barrier_semaphore()
    pl.semaphore_signal(barrier, inc=1, device_id=mate, device_id_type=MESH)
    pl.semaphore_signal(barrier, inc=1, device_id=across, device_id_type=MESH)

    @pl.when(z > 0)
    def _():
        pl.semaphore_signal(barrier, inc=1, device_id=left, device_id_type=MESH)

    @pl.when(z < Z - 1)
    def _():
        pl.semaphore_signal(barrier, inc=1, device_id=right, device_id_type=MESH)

    for ref in (l_a, l_b):
        ref[:, 0] = jnp.zeros_like(ref[:, 0])
    for ref in (r_a, r_b):
        ref[:, Z - 1] = jnp.zeros_like(ref[:, Z - 1])

    @pl.when((z > 0) & (z < Z - 1))
    def _():
        pl.semaphore_wait(barrier, 4)

    @pl.when((z == 0) | (z == Z - 1))
    def _():
        pl.semaphore_wait(barrier, 3)

    def remote(kind, q, src, dst, device):
        slot = lax.rem(q, SENDS)
        return pltpu.make_async_remote_copy(
            src_ref=src, dst_ref=dst, send_sem=send_sem.at[kind, slot], recv_sem=recv_sem.at[kind, slot], device_id=device, device_id_type=MESH
        )

    def local(kind, q, src, dst):
        return pltpu.make_async_copy(src, dst, local_sem.at[kind, lax.rem(q, SENDS)])

    def f(ref):
        return ref[...].astype(F32)

    def where(q):
        return lax.div(q, split), lax.rem(q, split)

    def by_weight(ml, act):
        for a in range(3):

            @pl.when(lax.div(ml, 2) == a)
            def _(a=a):
                act(a, lax.rem(ml, 2))

    class Part:
        def __init__(self, which):
            self.which = which
            self.base = 12 * which
            self.count = (big, small)[which]
            self.first = (0, big * split)[which]
            self.own, self.part, self.ry, self.rl, self.rr, self.sy, self.sl, self.sr = (
                (own_a, part_a, y_a, l_a, r_a, sy_a, sl_a, sr_a),
                (own_b, part_b, y_b, l_b, r_b, sy_b, sl_b, sr_b),
            )[which]
            self.w, self.m, self.v, self.nw, self.nm, self.nv = (
                (w_a, m_a, v_a, nw_a, nm_a, nv_a),
                (w_b, m_b, v_b, nw_b, nm_b, nv_b),
            )[which]

        def at(self, q):
            return pl.ds(self.first + lax.rem(q, split) * self.count, self.count)

        def remote(self, kind, q, src, dst, device):
            return remote(self.base + kind, q, src, dst, device)

        def local(self, kind, q, src, dst):
            return local(7 * self.which + kind, q, src, dst)

        def terms(self, q):
            slot = lax.rem(q, RING)

            def act(a, layer):
                self.remote(0, q, g[a].at[layer, :, :, other_c, self.at(q)], self.part.at[slot], mate).start()
                self.local(0, q, g[a].at[layer, :, :, c, self.at(q)], self.own.at[slot]).start()

            by_weight(where(q)[0], act)

        def terms_wait(self, q):
            slot = lax.rem(q, RING)
            self.local(0, q, self.own.at[slot], self.own.at[slot]).wait()
            self.remote(0, q, self.part.at[slot], self.part.at[slot], mate).wait_recv()

        def terms_sent(self, q):
            slot = lax.rem(q, RING)
            self.remote(0, q, self.part.at[slot], self.part.at[slot], mate).wait_send()

        def z_block(self, slot, j):
            raise NotImplementedError

        def z_send(self, q, h):
            slot, to = lax.rem(q, RING), lax.rem(q, SENDS)

            @pl.when(z == h - 1)
            def _():
                for j in range(h, Z):
                    self.z_sum(slot, j, self.sr.at[to, j], self.rl if h > 1 else None)
                self.remote(2, q, self.sr.at[to, h:Z], self.rl.at[slot, h:Z], right).start()

            @pl.when(z == Z - h)
            def _():
                for j in range(Z - h):
                    self.z_sum(slot, j, self.sl.at[to, j], self.rr if h > 1 else None)
                self.remote(3, q, self.sl.at[to, 0 : Z - h], self.rr.at[slot, 0 : Z - h], left).start()

        def z_wait(self, q, h):
            slot = lax.rem(q, RING)

            @pl.when(z == h)
            def _():
                self.remote(2, q, self.rl.at[slot, h:Z], self.rl.at[slot, h:Z], right).wait_recv()

            @pl.when(z == Z - 1 - h)
            def _():
                self.remote(3, q, self.rr.at[slot, 0 : Z - h], self.rr.at[slot, 0 : Z - h], left).wait_recv()

        def z_sent(self, q, h):
            to = lax.rem(q, SENDS)

            @pl.when(z == h - 1)
            def _():
                self.remote(2, q, self.sr.at[to, h:Z], self.sr.at[to, h:Z], right).wait_send()

            @pl.when(z == Z - h)
            def _():
                self.remote(3, q, self.sl.at[to, 0 : Z - h], self.sl.at[to, 0 : Z - h], left).wait_send()

        def state(self, q):
            slot = lax.rem(q, SENDS)

            def act(a, layer):
                self.local(1, q, w[a].at[layer, y, z, c, self.at(q)], self.w.at[slot]).start()
                self.local(2, q, m[a].at[layer, self.at(q)], self.m.at[slot]).start()
                self.local(3, q, v[a].at[layer, self.at(q)], self.v.at[slot]).start()

            by_weight(where(q)[0], act)

        def step(self, q, total):
            slot = lax.rem(q, SENDS)
            self.local(1, q, self.w.at[slot], self.w.at[slot]).wait()
            self.local(2, q, self.m.at[slot], self.m.at[slot]).wait()
            self.local(3, q, self.v.at[slot], self.v.at[slot]).wait()
            grad = total.astype(BF16).astype(F32)
            weight = f(self.w.at[slot])
            new_m = 0.9 * self.m[slot] + 0.1 * grad
            new_v = 0.95 * self.v[slot] + 0.05 * grad * grad
            self.nm[slot] = new_m
            self.nv[slot] = new_v
            self.nw[slot] = (weight - 0.02 * (new_m * lax.rsqrt(new_v + 1e-8) + 0.1 * weight)).astype(BF16)
            ml, _ = where(q)
            self.local(4, q, self.nw.at[slot], out.at[ml, y, z, c, self.at(q)]).start()
            self.local(5, q, self.nm.at[slot], moments.at[0, ml, self.at(q)]).start()
            self.local(6, q, self.nv.at[slot], moments.at[1, ml, self.at(q)]).start()

        def weight_stored(self, q):
            slot = lax.rem(q, SENDS)
            self.local(4, q, self.nw.at[slot], self.nw.at[slot]).wait()

        def moments_stored(self, q):
            slot = lax.rem(q, SENDS)
            self.local(5, q, self.nm.at[slot], self.nm.at[slot]).wait()
            self.local(6, q, self.nv.at[slot], self.nv.at[slot]).wait()

        def spread(self, q, h, src=None):
            @pl.when((z >= h) & (z < Z - 1))
            def _():
                dst = self.row(q, z - h)
                self.remote(5 + h, q, dst if src is None else src, dst, right).start()

            @pl.when((z + h < Z) & (z > 0))
            def _():
                dst = self.row(q, z + h)
                self.remote(8 + h, q, dst if src is None else src, dst, left).start()

        def spread_wait(self, q, h):
            @pl.when(z > h)
            def _():
                ref = self.row(q, z - h - 1)
                self.remote(5 + h, q, ref, ref, right).wait_recv()

            @pl.when(z + h + 1 < Z)
            def _():
                ref = self.row(q, z + h + 1)
                self.remote(8 + h, q, ref, ref, left).wait_recv()

        def spread_sent(self, q, h):
            @pl.when((z >= h) & (z < Z - 1))
            def _():
                ref = self.row(q, z - h)
                self.remote(5 + h, q, ref, ref, right).wait_send()

            @pl.when((z + h < Z) & (z > 0))
            def _():
                ref = self.row(q, z + h)
                self.remote(8 + h, q, ref, ref, left).wait_send()

        def share(self, q):
            ref = out.at[where(q)[0], :, :, c, self.at(q)]
            self.remote(11, q, ref, ref, mate).start()

        def share_wait(self, q):
            ref = out.at[where(q)[0], :, :, other_c, self.at(q)]
            self.remote(11, q, ref, ref, mate).wait_recv()

        def share_sent(self, q):
            ref = out.at[where(q)[0], :, :, c, self.at(q)]
            self.remote(11, q, ref, ref, mate).wait_send()

    class YFirst(Part):
        def row(self, q, j):
            return out.at[where(q)[0], y, j, c, self.at(q)]

        def z_sum(self, slot, j, to, more):
            total = f(self.own.at[slot, y, j]) + f(self.part.at[slot, y, j]) + f(self.ry.at[slot, j])
            to[...] = (total if more is None else total + f(more.at[slot, j])).astype(BF16)

        def y_send(self, q):
            slot, to = lax.rem(q, RING), lax.rem(q, SENDS)
            for j in range(Z):
                self.sy[to, j] = (f(self.own.at[slot, other_y, j]) + f(self.part.at[slot, other_y, j])).astype(BF16)
            self.remote(1, q, self.sy.at[to], self.ry.at[slot], across).start()

        def y_wait(self, q):
            slot = lax.rem(q, RING)
            self.remote(1, q, self.ry.at[slot], self.ry.at[slot], across).wait_recv()

        def y_sent(self, q):
            to = lax.rem(q, SENDS)
            self.remote(1, q, self.sy.at[to], self.sy.at[to], across).wait_send()

        def finish(self, q):
            slot = lax.rem(q, RING)
            total = f(self.own.at[slot, y, z]) + f(self.part.at[slot, y, z]) + f(self.ry.at[slot, z])
            self.step(q, total + f(self.rl.at[slot, z]) + f(self.rr.at[slot, z]))
            self.spread(q, 0, self.nw.at[lax.rem(q, SENDS)])

        def y_spread(self, q):
            ref = out.at[where(q)[0], y, :, c, self.at(q)]
            self.remote(4, q, ref, ref, across).start()

        def y_spread_wait(self, q):
            ref = out.at[where(q)[0], other_y, :, c, self.at(q)]
            self.remote(4, q, ref, ref, across).wait_recv()

        def y_spread_sent(self, q):
            ref = out.at[where(q)[0], y, :, c, self.at(q)]
            self.remote(4, q, ref, ref, across).wait_send()

    class ZFirst(Part):
        def row(self, q, j):
            return out.at[where(q)[0], :, j, c, self.at(q)]

        def z_sum(self, slot, j, to, more):
            for i in range(Y):
                total = f(self.own.at[slot, i, j]) + f(self.part.at[slot, i, j])
                to[i] = (total if more is None else total + f(more.at[slot, j, i])).astype(BF16)

        def column(self, slot, i):
            total = f(self.own.at[slot, i, z]) + f(self.part.at[slot, i, z])
            return total + f(self.rl.at[slot, z, i]) + f(self.rr.at[slot, z, i])

        def y_send(self, q):
            slot, to = lax.rem(q, RING), lax.rem(q, SENDS)
            self.sy[to] = self.column(slot, other_y).astype(BF16)
            self.remote(1, q, self.sy.at[to], self.ry.at[slot], across).start()

        def y_wait(self, q):
            slot = lax.rem(q, RING)
            self.remote(1, q, self.ry.at[slot], self.ry.at[slot], across).wait_recv()

        def y_sent(self, q):
            to = lax.rem(q, SENDS)
            self.remote(1, q, self.sy.at[to], self.sy.at[to], across).wait_send()

        def finish(self, q):
            slot = lax.rem(q, RING)
            self.step(q, self.column(slot, y) + f(self.ry.at[slot]))
            ref = out.at[where(q)[0], y, z, c, self.at(q)]
            self.remote(4, q, self.nw.at[lax.rem(q, SENDS)], ref, across).start()

        def y_spread_wait(self, q):
            ref = out.at[where(q)[0], other_y, z, c, self.at(q)]
            self.remote(4, q, ref, ref, across).wait_recv()

        def y_spread_sent(self, q):
            ref = out.at[where(q)[0], y, z, c, self.at(q)]
            self.remote(4, q, ref, ref, across).wait_send()

    a, b = YFirst(0), ZFirst(1)

    def iteration(t, _):
        def at(stage, *acts):
            q = t - stage

            @pl.when((q >= 0) & (q < n))
            def _():
                for act in acts:
                    act(q)

        def hop(act, h):
            return lambda q: act(q, h)

        at(0, a.terms, b.terms)
        at(0 + DRAIN, a.terms_sent, b.terms_sent)
        at(1 + DRAIN, a.y_sent, hop(b.z_sent, 1))
        at(2 + DRAIN, hop(a.z_sent, 1), hop(b.z_sent, 2))
        at(3 + DRAIN, hop(a.z_sent, 2), hop(b.z_sent, 3))
        at(4 + DRAIN, hop(a.z_sent, 3), b.y_sent)
        at(5 + DRAIN, hop(a.spread_sent, 0), b.y_spread_sent, a.moments_stored, b.moments_stored)
        at(6 + DRAIN, hop(a.spread_sent, 1), hop(b.spread_sent, 0))
        at(7 + DRAIN, hop(a.spread_sent, 2), hop(b.spread_sent, 1))
        at(8 + DRAIN, a.y_spread_sent, hop(b.spread_sent, 2))
        at(9 + DRAIN, a.share_sent, b.share_sent)
        at(3, a.state, b.state)
        at(1, a.terms_wait, a.y_send)
        at(8, hop(a.spread_wait, 2), a.y_spread)
        at(7, hop(a.spread_wait, 1), hop(a.spread, 2))
        at(6, a.weight_stored, hop(a.spread_wait, 0), hop(a.spread, 1))
        at(2, a.y_wait, hop(a.z_send, 1))
        at(3, hop(a.z_wait, 1), hop(a.z_send, 2))
        at(4, hop(a.z_wait, 2), hop(a.z_send, 3))
        at(5, hop(a.z_wait, 3), a.finish)
        at(9, a.y_spread_wait, a.share)
        at(1, b.terms_wait, hop(b.z_send, 1))
        at(8, hop(b.spread_wait, 1), hop(b.spread, 2))
        at(7, hop(b.spread_wait, 0), hop(b.spread, 1))
        at(6, b.weight_stored, b.y_spread_wait, hop(b.spread, 0))
        at(2, hop(b.z_wait, 1), hop(b.z_send, 2))
        at(3, hop(b.z_wait, 2), hop(b.z_send, 3))
        at(4, hop(b.z_wait, 3), b.y_send)
        at(5, b.y_wait, b.finish)
        at(9, hop(b.spread_wait, 2), b.share)
        at(10, a.share_wait, b.share_wait)
        return 0

    lax.fori_loop(0, n + LAST, iteration, 0)


def to_tiles(x, lead):
    *head, rows, columns = x.shape
    k = len(head)
    x = x.reshape(*head, rows // 8, 8, columns // 128, 128).transpose(*range(k), k, k + 2, k + 1, k + 3)
    return x.reshape(*lead, -1, 8, 128)


def from_tiles(x, shape):
    *head, rows, columns = shape
    k = len(head)
    x = x.reshape(*head, rows // 8, columns // 128, 8, 128).transpose(*range(k), k, k + 2, k + 1, k + 3)
    return x.reshape(shape)


def solution(mesh, split=SPLIT, options=None):
    def step(*arrays):
        terms, weights, m, v = (arrays[i : i + 3] for i in (0, 3, 6, 9))
        g = [to_tiles(t[0], (2, Y, Z, C)) for t in terms]
        w = [to_tiles(t, (2, Y, Z, C)) for t in weights]
        state = [to_tiles(t, (2,)) for t in (*m, *v)]
        tiles = state[0].shape[1]
        tile = (8, 128)

        def scratch(count):
            ring, sends = (RING,), (SENDS,)
            return ring, sends, (count, *tile)

        def buffers(count, line):
            one = (count, *tile)
            blocks = [(RING, Y, Z, *one)] * 2 + [(RING, *((Z,) if line == () else ()), *one)] + [(RING, Z, *line, *one)] * 2
            sent = [(SENDS, *((Z,) if line == () else ()), *one)] + [(SENDS, Z, *line, *one)] * 2
            return [pltpu.VMEM(shape, BF16) for shape in blocks + sent]

        big, small = 3 * tiles // 5 // split, 2 * tiles // 5 // split
        held = []
        for count in (big, small):
            held += [pltpu.VMEM((SENDS, count, *tile), t) for t in (BF16, F32, F32)]
        for count in (big, small):
            held += [pltpu.VMEM((SENDS, count, *tile), t) for t in (BF16, F32, F32)]
        out, moments = pl.pallas_call(
            functools.partial(kernel, split, tiles),
            out_shape=(
                jax.ShapeDtypeStruct((6, Y, Z, C, tiles, *tile), BF16),
                jax.ShapeDtypeStruct((2, 6, tiles, *tile), F32),
            ),
            in_specs=[pl.BlockSpec(memory_space=pl.ANY)] * 12,
            out_specs=(pl.BlockSpec(memory_space=pl.ANY),) * 2,
            scratch_shapes=[
                *buffers(big, ()),
                *buffers(small, (Y,)),
                *held,
                pltpu.SemaphoreType.DMA((14, SENDS)),
                pltpu.SemaphoreType.DMA((24, SENDS)),
                pltpu.SemaphoreType.DMA((24, SENDS)),
            ],
            compiler_params=pltpu.CompilerParams(collective_id=0, has_side_effects=True),
            name="step",
        )(*g, *w, *state)
        new = [from_tiles(out[2 * i : 2 * i + 2], t.shape) for i, t in enumerate(weights)]
        new_m = [from_tiles(moments[0, 2 * i : 2 * i + 2], t.shape) for i, t in enumerate(m)]
        new_v = [from_tiles(moments[1, 2 * i : 2 * i + 2], t.shape) for i, t in enumerate(v)]
        return (*new, *new_m, *new_v)

    all_of, cut = P(None, None, None), P(None, "dp", None)
    return jax.shard_map(
        step,
        mesh=mesh,
        in_specs=(P(("rep", "dp"), None, None, None),) * 3 + (all_of,) * 3 + (cut,) * 6,
        out_specs=(P("rep", None, None),) * 3 + (P("rep", "dp", None),) * 6,
        check_vma=False,
    )
```

time: 1030 us -> 562 us (0.55)
  waiting for transfers between devices: 951 us -> 0 us
  Pallas kernels: 0 us -> 504 us
  other arithmetic: 19.1 us -> 0 us
  local copies, waits for them, and re-layouts: 42.1 us -> 57 us
  between operations: 14.1 us -> 0.66 us
    reduce_scatter x3 -> x0, waiting for transfers between devices: 623 us -> none  [step(): lax.psum_scatter(t[0], 'dp', scatter_dimension=1, tiled=True)]
    pallas_call x0 -> x1, Pallas kernels: none -> 504 us  [step(): pl.pallas_call(functools.partial(kernel, split, tiles), out_shape=(jax.Sh...]
    all_gather x3 -> x0, waiting for transfers between devices: 325 us -> none  [step(): whole = [lax.all_gather(one[0], 'dp', axis=1, tiled=True) for one in new]]
    slice x0 -> x2, local copies, waits for them, and re-layouts: none -> 57 us  [the longest x1 45.7 us: step(): out[2 * i:2 * i + 2]]
    unnamed x19 -> x0, local copies, waits for them, and re-layouts: 42.1 us -> none
    convert_element_type x3 -> x0, other arithmetic: 19.1 us -> none  [adamw(): return ((w - 0.02 * step).astype(jnp.bfloat16), m, v)]
  transfers between devices with their start and end apart: 6 -> 0, of which waited for: 6 -> 0; matrix products, arithmetic and copies ran while one was open for 2% -> 0% of each run, Pallas kernels for 0% -> 0%
where the time goes in v1:
time: 562 us
  Pallas kernels  504 us (90%)
  local copies, waits for them, and re-layouts  57 us (10%)
    pallas_call x1, Pallas kernels, step(): pl.pallas_call(functools.partial(kernel, split, tiles), out_shape=(jax.Sh...  504 us
    slice x1, local copies, waits for them, and re-layouts, step(): out[2 * i:2 * i + 2]  45.7 us
    slice x1, local copies, waits for them, and re-layouts, step(): moments[1, 2 * i:2 * i + 2]  11.3 us

profile of v1, /device:TPU:0, one launch (start us, length us, event | category | flops | bytes accessed | tf_op | source)
XLA Modules:
  0.0 562.0 jit_solution(5045793362661020060)
XLA Ops:
  0.6 504.4 %step.1 = (bf16[6,2,4,2,320,8,128]{6,5,4,3,2,1,0:T(8,128)(2,1)}, f32[2,6,320,8,128]{4,3,2,1,0:T(8,128)}) custom-call(bf16[2,2,4,2,320,8,128]{6,5,4,3,2,1,0:T(8,128)(2,1)} %bitcast.105, bf16[2,2,4,2,320,8,128]{6,5,4,3,2,1,0:T(8,128)(2,1)} %bitcast.106, bf16[2,2,4,2,320,8,128]{6,5,4,3,2,1,0:T(8,128)(2,1)} %bitcast.107, ...), custom_call_target="tpu_custom_call" | custom-call | tf_op jit(solution)/shard_map/step/pallas_call | solution.py:415
  505.1 45.7 %fusion = (bf16[2,2,4,2,320,8,128]{6,5,4,3,2,1,0:T(8,128)(2,1)}, bf16[2,2,4,2,320,8,128]{6,5,4,3,2,1,0:T(8,128)(2,1)}, bf16[2,2,4,2,320,8,128]{6,5,4,3,2,1,0:T(8,128)(2,1)}) fusion(bf16[6,2,4,2,320,8,128]{6,5,4,3,2,1,0:T(8,128)(2,1)} %get-tuple-element.11), kind=kLoop, calls=%fused_computation | loop fusion | bytes 125829120 | tf_op jit(solution)/shard_map/slice | solution.py:434
  550.7 11.3 %fusion.1 = (f32[1,2,320,8,128]{4,3,2,1,0:T(8,128)}, f32[1,2,320,8,128]{4,3,2,1,0:T(8,128)}, f32[1,2,320,8,128]{4,3,2,1,0:T(8,128)}, f32[1,2,320,8,128]{4,3,2,1,...) fusion(f32[2,6,320,8,128]{4,3,2,1,0:T(8,128)} %get-tuple-element.12), kind=kLoop, calls=%fused_computation.1 | loop fusion | bytes 31457280 | tf_op jit(solution)/shard_map/slice | solution.py:436

commit v2 on v1

--- a/solution.py
+++ b/solution.py
@@ -15,14 +15,17 @@
 SENDS = 4
 DRAIN = 2
 LAST = 10 + DRAIN
+FAR = 3
+DEPTH = 4
+VMEM_BYTES = 67_043_328
 
 
 def kernel(split, tiles, *refs):
     g, w, m, v = (refs[i : i + 3] for i in (0, 3, 6, 9))
-    out, moments = refs[12:14]
-    (own_a, part_a, y_a, l_a, r_a, sy_a, sl_a, sr_a, own_b, part_b, y_b, l_b, r_b, sy_b, sl_b, sr_b) = refs[14:30]
-    (w_a, m_a, v_a, w_b, m_b, v_b, nw_a, nm_a, nv_a, nw_b, nm_b, nv_b) = refs[30:42]
-    local_sem, send_sem, recv_sem = refs[42:45]
+    far, near, moments = refs[12:15]
+    (own_a, part_a, y_a, l_a, r_a, sy_a, sl_a, sr_a, own_b, part_b, y_b, l_b, r_b, sy_b, sl_b, sr_b) = refs[15:31]
+    (w_a, m_a, v_a, nw_a, w_b, m_b, v_b, nw_b) = refs[31:39]
+    local_sem, send_sem, recv_sem = refs[39:42]
 
     me = lax.axis_index("dp")
     c, z, y = lax.rem(me, C), lax.rem(lax.div(me, C), Z), lax.div(me, C * Z)
@@ -79,6 +82,17 @@
             @pl.when(lax.div(ml, 2) == a)
             def _(a=a):
                 act(a, lax.rem(ml, 2))
+
+    def placed(q, act):
+        ml = lax.div(q, split)
+
+        @pl.when(ml < FAR)
+        def _():
+            act(far.at[ml])
+
+        @pl.when(ml >= FAR)
+        def _():
+            act(near.at[ml - FAR])
 
     class Part:
         def __init__(self, which):
@@ -90,10 +104,7 @@
                 (own_a, part_a, y_a, l_a, r_a, sy_a, sl_a, sr_a),
                 (own_b, part_b, y_b, l_b, r_b, sy_b, sl_b, sr_b),
             )[which]
-            self.w, self.m, self.v, self.nw, self.nm, self.nv = (
-                (w_a, m_a, v_a, nw_a, nm_a, nv_a),
-                (w_b, m_b, v_b, nw_b, nm_b, nv_b),
-            )[which]
+            self.w, self.m, self.v, self.nw = ((w_a, m_a, v_a, nw_a), (w_b, m_b, v_b, nw_b))[which]
 
         def at(self, q):
             return pl.ds(self.first + lax.rem(q, split) * self.count, self.count)
@@ -102,7 +113,7 @@
             return remote(self.base + kind, q, src, dst, device)
 
         def local(self, kind, q, src, dst):
-            return local(7 * self.which + kind, q, src, dst)
+            return local(5 * self.which + kind, q, src, dst)
 
         def terms(self, q):
             slot = lax.rem(q, RING)
@@ -181,71 +192,93 @@
             weight = f(self.w.at[slot])
             new_m = 0.9 * self.m[slot] + 0.1 * grad
             new_v = 0.95 * self.v[slot] + 0.05 * grad * grad
-            self.nm[slot] = new_m
-            self.nv[slot] = new_v
-            self.nw[slot] = (weight - 0.02 * (new_m * lax.rsqrt(new_v + 1e-8) + 0.1 * weight)).astype(BF16)
             ml, _ = where(q)
-            self.local(4, q, self.nw.at[slot], out.at[ml, y, z, c, self.at(q)]).start()
-            self.local(5, q, self.nm.at[slot], moments.at[0, ml, self.at(q)]).start()
-            self.local(6, q, self.nv.at[slot], moments.at[1, ml, self.at(q)]).start()
+            moments[0, ml, self.at(q)] = new_m
+            moments[1, ml, self.at(q)] = new_v
+            new_w = (weight - 0.02 * (new_m * lax.rsqrt(new_v + 1e-8) + 0.1 * weight)).astype(BF16)
+            self.nw[slot] = new_w
+
+            @pl.when(ml < FAR)
+            def _():
+                self.local(4, q, self.nw.at[slot], far.at[ml, y, z, c, self.at(q)]).start()
+
+            @pl.when(ml >= FAR)
+            def _():
+                near[ml - FAR, y, z, c, self.at(q)] = new_w
 
         def weight_stored(self, q):
             slot = lax.rem(q, SENDS)
-            self.local(4, q, self.nw.at[slot], self.nw.at[slot]).wait()
-
-        def moments_stored(self, q):
-            slot = lax.rem(q, SENDS)
-            self.local(5, q, self.nm.at[slot], self.nm.at[slot]).wait()
-            self.local(6, q, self.nv.at[slot], self.nv.at[slot]).wait()
+
+            @pl.when(where(q)[0] < FAR)
+            def _():
+                self.local(4, q, self.nw.at[slot], self.nw.at[slot]).wait()
 
         def spread(self, q, h, src=None):
-            @pl.when((z >= h) & (z < Z - 1))
-            def _():
-                dst = self.row(q, z - h)
-                self.remote(5 + h, q, dst if src is None else src, dst, right).start()
-
-            @pl.when((z + h < Z) & (z > 0))
-            def _():
-                dst = self.row(q, z + h)
-                self.remote(8 + h, q, dst if src is None else src, dst, left).start()
+            def act(o):
+                @pl.when((z >= h) & (z < Z - 1))
+                def _():
+                    dst = self.row(o, q, z - h)
+                    self.remote(5 + h, q, dst if src is None else src, dst, right).start()
+
+                @pl.when((z + h < Z) & (z > 0))
+                def _():
+                    dst = self.row(o, q, z + h)
+                    self.remote(8 + h, q, dst if src is None else src, dst, left).start()
+
+            placed(q, act)
 
         def spread_wait(self, q, h):
-            @pl.when(z > h)
-            def _():
-                ref = self.row(q, z - h - 1)
-                self.remote(5 + h, q, ref, ref, right).wait_recv()
-
-            @pl.when(z + h + 1 < Z)
-            def _():
-                ref = self.row(q, z + h + 1)
-                self.remote(8 + h, q, ref, ref, left).wait_recv()
+            def act(o):
+                @pl.when(z > h)
+                def _():
+                    ref = self.row(o, q, z - h - 1)
+                    self.remote(5 + h, q, ref, ref, right).wait_recv()
+
+                @pl.when(z + h + 1 < Z)
+                def _():
+                    ref = self.row(o, q, z + h + 1)
+                    self.remote(8 + h, q, ref, ref, left).wait_recv()
+
+            placed(q, act)
 
         def spread_sent(self, q, h):
-            @pl.when((z >= h) & (z < Z - 1))
-            def _():
-                ref = self.row(q, z - h)
-                self.remote(5 + h, q, ref, ref, right).wait_send()
-
-            @pl.when((z + h < Z) & (z > 0))
-            def _():
-                ref = self.row(q, z + h)
-                self.remote(8 + h, q, ref, ref, left).wait_send()
+            def act(o):
+                @pl.when((z >= h) & (z < Z - 1))
+                def _():
+                    ref = self.row(o, q, z - h)
+                    self.remote(5 + h, q, ref, ref, right).wait_send()
+
+                @pl.when((z + h < Z) & (z > 0))
+                def _():
+                    ref = self.row(o, q, z + h)
+                    self.remote(8 + h, q, ref, ref, left).wait_send()
+
+            placed(q, act)
 
         def share(self, q):
-            ref = out.at[where(q)[0], :, :, c, self.at(q)]
-            self.remote(11, q, ref, ref, mate).start()
+            def act(o):
+                ref = o.at[:, :, c, self.at(q)]
+                self.remote(11, q, ref, ref, mate).start()
+
+            placed(q, act)
 
         def share_wait(self, q):
-            ref = out.at[where(q)[0], :, :, other_c, self.at(q)]
-            self.remote(11, q, ref, ref, mate).wait_recv()
+            def act(o):
+                ref = o.at[:, :, other_c, self.at(q)]
+                self.remote(11, q, ref, ref, mate).wait_recv()
+
+            placed(q, act)
 
         def share_sent(self, q):
-            ref = out.at[where(q)[0], :, :, c, self.at(q)]
-            self.remote(11, q, ref, ref, mate).wait_send()
+            def act(o):
+                ref = o.at[:, :, c, self.at(q)]
+                self.remote(11, q, ref, ref, mate).wait_send()
+
+            placed(q, act)
 
     class YFirst(Part):
-        def row(self, q, j):
-            return out.at[where(q)[0], y, j, c, self.at(q)]
+        def row(self, o, q, j):
+            return o.at[y, j, c, self.at(q)]
 
         def z_sum(self, slot, j, to, more):
             total = f(self.own.at[slot, y, j]) + f(self.part.at[slot, y, j]) + f(self.ry.at[slot, j])
@@ -272,20 +305,29 @@
             self.spread(q, 0, self.nw.at[lax.rem(q, SENDS)])
 
         def y_spread(self, q):
-            ref = out.at[where(q)[0], y, :, c, self.at(q)]
-            self.remote(4, q, ref, ref, across).start()
+            def act(o):
+                ref = o.at[y, :, c, self.at(q)]
+                self.remote(4, q, ref, ref, across).start()
+
+            placed(q, act)
 
         def y_spread_wait(self, q):
-            ref = out.at[where(q)[0], other_y, :, c, self.at(q)]
-            self.remote(4, q, ref, ref, across).wait_recv()
+            def act(o):
+                ref = o.at[other_y, :, c, self.at(q)]
+                self.remote(4, q, ref, ref, across).wait_recv()
+
+            placed(q, act)
 
         def y_spread_sent(self, q):
-            ref = out.at[where(q)[0], y, :, c, self.at(q)]
-            self.remote(4, q, ref, ref, across).wait_send()
+            def act(o):
+                ref = o.at[y, :, c, self.at(q)]
+                self.remote(4, q, ref, ref, across).wait_send()
+
+            placed(q, act)
 
     class ZFirst(Part):
-        def row(self, q, j):
-            return out.at[where(q)[0], :, j, c, self.at(q)]
+        def row(self, o, q, j):
+            return o.at[:, j, c, self.at(q)]
 
         def z_sum(self, slot, j, to, more):
             for i in range(Y):
@@ -312,16 +354,25 @@
         def finish(self, q):
             slot = lax.rem(q, RING)
             self.step(q, self.column(slot, y) + f(self.ry.at[slot]))
-            ref = out.at[where(q)[0], y, z, c, self.at(q)]
-            self.remote(4, q, self.nw.at[lax.rem(q, SENDS)], ref, across).start()
+
+            def act(o):
+                self.remote(4, q, self.nw.at[lax.rem(q, SENDS)], o.at[y, z, c, self.at(q)], across).start()
+
+            placed(q, act)
 
         def y_spread_wait(self, q):
-            ref = out.at[where(q)[0], other_y, z, c, self.at(q)]
-            self.remote(4, q, ref, ref, across).wait_recv()
+            def act(o):
+                ref = o.at[other_y, z, c, self.at(q)]
+                self.remote(4, q, ref, ref, across).wait_recv()
+
+            placed(q, act)
 
         def y_spread_sent(self, q):
-            ref = out.at[where(q)[0], y, z, c, self.at(q)]
-            self.remote(4, q, ref, ref, across).wait_send()
+            def act(o):
+                ref = o.at[y, z, c, self.at(q)]
+                self.remote(4, q, ref, ref, across).wait_send()
+
+            placed(q, act)
 
     a, b = YFirst(0), ZFirst(1)
 
@@ -343,7 +394,7 @@
         at(2 + DRAIN, hop(a.z_sent, 1), hop(b.z_sent, 2))
         at(3 + DRAIN, hop(a.z_sent, 2), hop(b.z_sent, 3))
         at(4 + DRAIN, hop(a.z_sent, 3), b.y_sent)
-        at(5 + DRAIN, hop(a.spread_sent, 0), b.y_spread_sent, a.moments_stored, b.moments_stored)
+        at(5 + DRAIN, hop(a.spread_sent, 0), b.y_spread_sent)
         at(6 + DRAIN, hop(a.spread_sent, 1), hop(b.spread_sent, 0))
         at(7 + DRAIN, hop(a.spread_sent, 2), hop(b.spread_sent, 1))
         at(8 + DRAIN, a.y_spread_sent, hop(b.spread_sent, 2))
@@ -373,6 +424,37 @@
     lax.fori_loop(0, n + LAST, iteration, 0)
 
 
+def store(far, near, moments, *refs):
+    new, states, (line, read_sem, write_sem, held_sem) = refs[:3], refs[3:9], refs[9:]
+    pieces = [(ml, j) for ml in range(FAR) for j in range(Y * Z)]
+
+    def read(i):
+        ml, j = pieces[i]
+        return pltpu.make_async_copy(far.at[ml, j // Z, j % Z], line.at[i % DEPTH], read_sem.at[i % DEPTH])
+
+    def write(i):
+        ml, j = pieces[i]
+        return pltpu.make_async_copy(line.at[i % DEPTH], new[ml // 2].at[ml % 2, j // Z, j % Z], write_sem.at[i % DEPTH])
+
+    held = [(near.at[ml - FAR], new[ml // 2].at[ml % 2]) for ml in range(FAR, 6)]
+    held += [(moments.at[i // 3, 2 * (i % 3) : 2 * (i % 3) + 2], states[i]) for i in range(6)]
+    held = [pltpu.make_async_copy(src, dst, held_sem.at[i]) for i, (src, dst) in enumerate(held)]
+    for i in range(DEPTH):
+        read(i).start()
+    for copy in held:
+        copy.start()
+    for i in range(len(pieces)):
+        read(i).wait()
+        write(i).start()
+        if i >= 1 and i - 1 + DEPTH < len(pieces):
+            write(i - 1).wait()
+            read(i - 1 + DEPTH).start()
+    for i in range(len(pieces) - DEPTH, len(pieces)):
+        write(i).wait()
+    for copy in held:
+        copy.wait()
+
+
 def to_tiles(x, lead):
     *head, rows, columns = x.shape
     k = len(head)
@@ -387,7 +469,7 @@
     return x.reshape(shape)
 
 
-def solution(mesh, split=SPLIT, options=None):
+def solution(mesh, split=SPLIT):
     def step(*arrays):
         terms, weights, m, v = (arrays[i : i + 3] for i in (0, 3, 6, 9))
         g = [to_tiles(t[0], (2, Y, Z, C)) for t in terms]
@@ -395,10 +477,7 @@
         state = [to_tiles(t, (2,)) for t in (*m, *v)]
         tiles = state[0].shape[1]
         tile = (8, 128)
-
-        def scratch(count):
-            ring, sends = (RING,), (SENDS,)
-            return ring, sends, (count, *tile)
+        limit = VMEM_BYTES - 1024 * tiles * (2 * Y * Z * C * (6 - FAR) + 4 * 2 * 6)
 
         def buffers(count, line):
             one = (count, *tile)
@@ -407,34 +486,41 @@
             return [pltpu.VMEM(shape, BF16) for shape in blocks + sent]
 
         big, small = 3 * tiles // 5 // split, 2 * tiles // 5 // split
-        held = []
-        for count in (big, small):
-            held += [pltpu.VMEM((SENDS, count, *tile), t) for t in (BF16, F32, F32)]
-        for count in (big, small):
-            held += [pltpu.VMEM((SENDS, count, *tile), t) for t in (BF16, F32, F32)]
-        out, moments = pl.pallas_call(
+        held = [pltpu.VMEM((SENDS, count, *tile), t) for count in (big, small) for t in (BF16, F32, F32, BF16)]
+        whole = (Y, Z, C, tiles, *tile)
+        hbm, vmem = pl.BlockSpec(memory_space=pltpu.HBM), pl.BlockSpec(memory_space=pltpu.VMEM)
+        far, near, moments = pl.pallas_call(
             functools.partial(kernel, split, tiles),
-            out_shape=(
-                jax.ShapeDtypeStruct((6, Y, Z, C, tiles, *tile), BF16),
-                jax.ShapeDtypeStruct((2, 6, tiles, *tile), F32),
-            ),
+            out_shape=(pltpu.HBM((FAR, *whole), BF16), pltpu.VMEM((6 - FAR, *whole), BF16), pltpu.VMEM((2, 6, tiles, *tile), F32)),
             in_specs=[pl.BlockSpec(memory_space=pl.ANY)] * 12,
-            out_specs=(pl.BlockSpec(memory_space=pl.ANY),) * 2,
+            out_specs=(hbm, vmem, vmem),
             scratch_shapes=[
                 *buffers(big, ()),
                 *buffers(small, (Y,)),
                 *held,
-                pltpu.SemaphoreType.DMA((14, SENDS)),
+                pltpu.SemaphoreType.DMA((10, SENDS)),
                 pltpu.SemaphoreType.DMA((24, SENDS)),
                 pltpu.SemaphoreType.DMA((24, SENDS)),
             ],
-            compiler_params=pltpu.CompilerParams(collective_id=0, has_side_effects=True),
+            compiler_params=pltpu.CompilerParams(collective_id=0, has_side_effects=True, vmem_limit_bytes=limit),
             name="step",
         )(*g, *w, *state)
-        new = [from_tiles(out[2 * i : 2 * i + 2], t.shape) for i, t in enumerate(weights)]
-        new_m = [from_tiles(moments[0, 2 * i : 2 * i + 2], t.shape) for i, t in enumerate(m)]
-        new_v = [from_tiles(moments[1, 2 * i : 2 * i + 2], t.shape) for i, t in enumerate(v)]
-        return (*new, *new_m, *new_v)
+        near, moments = (pltpu.with_memory_space_constraint(x, pltpu.VMEM) for x in (near, moments))
+        results = pl.pallas_call(
+            store,
+            out_shape=[jax.ShapeDtypeStruct((2, *whole), BF16)] * 3 + [jax.ShapeDtypeStruct((2, tiles, *tile), F32)] * 6,
+            in_specs=[hbm, vmem, vmem],
+            out_specs=[pl.BlockSpec(memory_space=pl.ANY)] * 9,
+            scratch_shapes=[
+                pltpu.VMEM((DEPTH, C, tiles, *tile), BF16),
+                pltpu.SemaphoreType.DMA((DEPTH,)),
+                pltpu.SemaphoreType.DMA((DEPTH,)),
+                pltpu.SemaphoreType.DMA((12 - FAR,)),
+            ],
+            compiler_params=pltpu.CompilerParams(vmem_limit_bytes=limit),
+            name="store",
+        )(far, near, moments)
+        return tuple(from_tiles(x, t.shape) for x, t in zip(results, (*weights, *m, *v), strict=True))
 
     all_of, cut = P(None, None, None), P(None, "dp", None)
     return jax.shard_map(

time: 562 us -> 541 us (0.963)
  local copies, waits for them, and re-layouts: 57 us -> 0 us
  Pallas kernels: 504 us -> 540 us
    slice x2 -> x0, local copies, waits for them, and re-layouts: 57 us -> none  [the longest x1 45.7 us: step(): out[2 * i:2 * i + 2]]
    pallas_call x1 -> x2, Pallas kernels: 504 us -> 540 us  [the longest x1 504 us: step(): pl.pallas_call(functools.partial(kernel, split, tiles), out_shape=(pltpu....]
where the time goes in v2:
time: 541 us
  Pallas kernels  540 us (100%)
    pallas_call x1, Pallas kernels, step(): pl.pallas_call(functools.partial(kernel, split, tiles), out_shape=(pltpu....  504 us
    pallas_call x1, Pallas kernels, step(): pl.pallas_call(store, out_shape=[jax.ShapeDtypeStruct((2, *whole), BF16)]...  36.2 us

profile of v2, /device:TPU:0, one launch (start us, length us, event | category | flops | bytes accessed | tf_op | source)
XLA Modules:
  0.0 541.1 jit_solution(13103651747722843248)
XLA Ops:
  0.6 504.3 %step.1 = (bf16[3,2,4,2,320,8,128]{6,5,4,3,2,1,0:T(8,128)(2,1)}, bf16[3,2,4,2,320,8,128]{6,5,4,3,2,1,0:T(8,128)(2,1)S(1)}, f32[2,6,320,8,128]{4,3,2,1,0:T(8,128)S(1)}) custom-call(bf16[2,2,4,2,320,8,128]{6,5,4,3,2,1,0:T(8,128)(2,1)} %bitcast.105, bf16[2,2,4,2,320,8,128]{6,5,4,3,2,1,0:T(8,128)(2,1)} %bitcast.106, ...), custom_call_target="tpu_custom_call" | custom-call | tf_op jit(solution)/shard_map/step/pallas_call | solution.py:492
  504.9 36.2 %store.1 = (bf16[2,2,4,2,320,8,128]{6,5,4,3,2,1,0:T(8,128)(2,1)}, bf16[2,2,4,2,320,8,128]{6,5,4,3,2,1,0:T(8,128)(2,1)}, bf16[2,2,4,2,320,8,128]{6,5,4,3,2,1,0:T(...) custom-call(bf16[3,2,4,2,320,8,128]{6,5,4,3,2,1,0:T(8,128)(2,1)} %ge, ...), custom_call_target="tpu_custom_call" | custom-call | tf_op jit(solution)/shard_map/store/pallas_call | solution.py:509

commit v3 on v2

--- a/solution.py
+++ b/solution.py
@@ -22,10 +22,10 @@
 
 def kernel(split, tiles, *refs):
     g, w, m, v = (refs[i : i + 3] for i in (0, 3, 6, 9))
-    far, near, moments = refs[12:15]
-    (own_a, part_a, y_a, l_a, r_a, sy_a, sl_a, sr_a, own_b, part_b, y_b, l_b, r_b, sy_b, sl_b, sr_b) = refs[15:31]
-    (w_a, m_a, v_a, nw_a, w_b, m_b, v_b, nw_b) = refs[31:39]
-    local_sem, send_sem, recv_sem = refs[39:42]
+    far, near, moments, ahead, own_a, part_a, own_b, part_b = refs[12:20]
+    (y_a, l_a, r_a, sy_a, sl_a, sr_a, y_b, l_b, r_b, sy_b, sl_b, sr_b) = refs[20:32]
+    (w_a, m_a, v_a, nw_a, w_b, m_b, v_b, nw_b) = refs[32:40]
+    local_sem, send_sem, recv_sem, ahead_sem = refs[40:44]
 
     me = lax.axis_index("dp")
     c, z, y = lax.rem(me, C), lax.rem(lax.div(me, C), Z), lax.div(me, C * Z)
@@ -375,6 +375,11 @@
             placed(q, act)
 
     a, b = YFirst(0), ZFirst(1)
+
+    def early():
+        source = far.at[FAR - 1]
+        pairs = held_pieces(split, tiles, source, (ahead, own_a, part_a, own_b, part_b))
+        return [pltpu.make_async_copy(src, dst, ahead_sem.at[i]) for i, (src, dst) in enumerate(pairs)]
 
     def iteration(t, _):
         def at(stage, *acts):
@@ -419,14 +424,35 @@
         at(5, b.y_wait, b.finish)
         at(9, hop(b.spread_wait, 2), b.share)
         at(10, a.share_wait, b.share_wait)
+
+        @pl.when(t == n + 5)
+        def _():
+            for copy in early():
+                copy.start()
+
         return 0
 
     lax.fori_loop(0, n + LAST, iteration, 0)
-
-
-def store(far, near, moments, *refs):
-    new, states, (line, read_sem, write_sem, held_sem) = refs[:3], refs[3:9], refs[9:]
-    pieces = [(ml, j) for ml in range(FAR) for j in range(Y * Z)]
+    for copy in early():
+        copy.wait()
+
+
+def held_pieces(split, tiles, whole, held):
+    ahead, *slots = held
+    pairs = [(whole.at[:, :, 1], ahead)]
+    first = 0
+    for own, part in (slots[:2], slots[2:]):
+        count = own.shape[3]
+        for r in range(split):
+            piece = whole.at[:, :, 0, first + r * count : first + (r + 1) * count]
+            pairs.append((piece, (own if r < RING else part).at[r % RING]))
+        first += count * split
+    return pairs
+
+
+def store(split, tiles, far, near, moments, *refs):
+    early, new, states, (line, read_sem, write_sem, held_sem) = refs[:5], refs[5:8], refs[8:14], refs[14:]
+    pieces = [(ml, j) for ml in range(FAR - 1) for j in range(Y * Z)]
 
     def read(i):
         ml, j = pieces[i]
@@ -438,6 +464,7 @@
 
     held = [(near.at[ml - FAR], new[ml // 2].at[ml % 2]) for ml in range(FAR, 6)]
     held += [(moments.at[i // 3, 2 * (i % 3) : 2 * (i % 3) + 2], states[i]) for i in range(6)]
+    held += [(src, dst) for dst, src in held_pieces(split, tiles, new[(FAR - 1) // 2].at[(FAR - 1) % 2], early)]
     held = [pltpu.make_async_copy(src, dst, held_sem.at[i]) for i, (src, dst) in enumerate(held)]
     for i in range(DEPTH):
         read(i).start()
@@ -477,11 +504,12 @@
         state = [to_tiles(t, (2,)) for t in (*m, *v)]
         tiles = state[0].shape[1]
         tile = (8, 128)
-        limit = VMEM_BYTES - 1024 * tiles * (2 * Y * Z * C * (6 - FAR) + 4 * 2 * 6)
+        limit = VMEM_BYTES - 1024 * tiles * (2 * Y * Z * C * (6 - FAR) + 4 * 2 * 6 + 2 * Y * Z)
+        limit -= 2 * 1024 * 2 * RING * Y * Z * tiles // split
 
         def buffers(count, line):
             one = (count, *tile)
-            blocks = [(RING, Y, Z, *one)] * 2 + [(RING, *((Z,) if line == () else ()), *one)] + [(RING, Z, *line, *one)] * 2
+            blocks = [(RING, *((Z,) if line == () else ()), *one)] + [(RING, Z, *line, *one)] * 2
             sent = [(SENDS, *((Z,) if line == () else ()), *one)] + [(SENDS, Z, *line, *one)] * 2
             return [pltpu.VMEM(shape, BF16) for shape in blocks + sent]
 
@@ -489,11 +517,18 @@
         held = [pltpu.VMEM((SENDS, count, *tile), t) for count in (big, small) for t in (BF16, F32, F32, BF16)]
         whole = (Y, Z, C, tiles, *tile)
         hbm, vmem = pl.BlockSpec(memory_space=pltpu.HBM), pl.BlockSpec(memory_space=pltpu.VMEM)
-        far, near, moments = pl.pallas_call(
+        terms_of = [(RING, Y, Z, count, *tile) for count in (big, big, small, small)]
+        far, *kept = pl.pallas_call(
             functools.partial(kernel, split, tiles),
-            out_shape=(pltpu.HBM((FAR, *whole), BF16), pltpu.VMEM((6 - FAR, *whole), BF16), pltpu.VMEM((2, 6, tiles, *tile), F32)),
+            out_shape=(
+                pltpu.HBM((FAR, *whole), BF16),
+                pltpu.VMEM((6 - FAR, *whole), BF16),
+                pltpu.VMEM((2, 6, tiles, *tile), F32),
+                pltpu.VMEM((Y, Z, tiles, *tile), BF16),
+                *(pltpu.VMEM(shape, BF16) for shape in terms_of),
+            ),
             in_specs=[pl.BlockSpec(memory_space=pl.ANY)] * 12,
-            out_specs=(hbm, vmem, vmem),
+            out_specs=(hbm,) + (vmem,) * 7,
             scratch_shapes=[
                 *buffers(big, ()),
                 *buffers(small, (Y,)),
@@ -501,25 +536,26 @@
                 pltpu.SemaphoreType.DMA((10, SENDS)),
                 pltpu.SemaphoreType.DMA((24, SENDS)),
                 pltpu.SemaphoreType.DMA((24, SENDS)),
+                pltpu.SemaphoreType.DMA((1 + 2 * split,)),
             ],
             compiler_params=pltpu.CompilerParams(collective_id=0, has_side_effects=True, vmem_limit_bytes=limit),
             name="step",
         )(*g, *w, *state)
-        near, moments = (pltpu.with_memory_space_constraint(x, pltpu.VMEM) for x in (near, moments))
+        kept = [pltpu.with_memory_space_constraint(x, pltpu.VMEM) for x in kept]
         results = pl.pallas_call(
-            store,
+            functools.partial(store, split, tiles),
             out_shape=[jax.ShapeDtypeStruct((2, *whole), BF16)] * 3 + [jax.ShapeDtypeStruct((2, tiles, *tile), F32)] * 6,
-            in_specs=[hbm, vmem, vmem],
+            in_specs=[hbm] + [vmem] * 7,
             out_specs=[pl.BlockSpec(memory_space=pl.ANY)] * 9,
             scratch_shapes=[
                 pltpu.VMEM((DEPTH, C, tiles, *tile), BF16),
                 pltpu.SemaphoreType.DMA((DEPTH,)),
                 pltpu.SemaphoreType.DMA((DEPTH,)),
-                pltpu.SemaphoreType.DMA((12 - FAR,)),
+                pltpu.SemaphoreType.DMA((13 - FAR + 2 * split,)),
             ],
             compiler_params=pltpu.CompilerParams(vmem_limit_bytes=limit),
             name="store",
-        )(far, near, moments)
+        )(far, *kept)
         return tuple(from_tiles(x, t.shape) for x, t in zip(results, (*weights, *m, *v), strict=True))
 
     all_of, cut = P(None, None, None), P(None, "dp", None)

time: 541 us -> 539 us (level)
  no operation moved by 1% of the time
where the time goes in v3:
time: 539 us; the launch traced here: 538 us
  Pallas kernels  538 us (100%)
    pallas_call x1, Pallas kernels, step(): pl.pallas_call(functools.partial(kernel, split, tiles), out_shape=(pltpu....  505 us
    pallas_call x1, Pallas kernels, step(): pl.pallas_call(functools.partial(store, split, tiles), out_shape=[jax.Sha...  33.1 us

profile of v3, /device:TPU:0, one launch (start us, length us, event | category | flops | bytes accessed | tf_op | source)
XLA Modules:
  0.0 538.4 jit_solution(10883761232589446223)
XLA Ops:
  0.6 504.6 %step.1 = (bf16[3,2,4,2,320,8,128]{6,5,4,3,2,1,0:T(8,128)(2,1)}, bf16[3,2,4,2,320,8,128]{6,5,4,3,2,1,0:T(8,128)(2,1)S(1)}, f32[2,6,320,8,128]{4,3,2,1,0:T(8,128)...) custom-call(bf16[2,2,4,2,320,8,128]{6,5,4,3,2,1,0:T(8,128)(2,1)} %bi, ...), custom_call_target="tpu_custom_call" | custom-call | tf_op jit(solution)/shard_map/step/pallas_call | solution.py:521
  505.3 33.1 %store.1 = (bf16[2,2,4,2,320,8,128]{6,5,4,3,2,1,0:T(8,128)(2,1)}, bf16[2,2,4,2,320,8,128]{6,5,4,3,2,1,0:T(8,128)(2,1)}, bf16[2,2,4,2,320,8,128]{6,5,4,3,2,1,0:T(...) custom-call(bf16[3,2,4,2,320,8,128]{6,5,4,3,2,1,0:T(8,128)(2,1)} %ge, ...), custom_call_target="tpu_custom_call" | custom-call | tf_op jit(solution)/shard_map/store/pallas_call | solution.py:545

commit v4 on v3

--- a/solution.py
+++ b/solution.py
@@ -13,8 +13,10 @@
 SPLIT = 16
 RING = 8
 SENDS = 4
+SEMS = 8
 DRAIN = 2
-LAST = 10 + DRAIN
+SHORT = 2
+LAST = 9
 FAR = 3
 DEPTH = 4
 VMEM_BYTES = 67_043_328
@@ -62,7 +64,7 @@
         pl.semaphore_wait(barrier, 3)
 
     def remote(kind, q, src, dst, device):
-        slot = lax.rem(q, SENDS)
+        slot = lax.rem(q, SEMS)
         return pltpu.make_async_remote_copy(
             src_ref=src, dst_ref=dst, send_sem=send_sem.at[kind, slot], recv_sem=recv_sem.at[kind, slot], device_id=device, device_id_type=MESH
         )
@@ -255,6 +257,40 @@
 
             placed(q, act)
 
+        def straight(self, q, src=None):
+            def act(o):
+                ref = self.row(o, q, z)
+                for h in range(Z - 1):
+
+                    @pl.when(z + h + 1 < Z)
+                    def _(h=h):
+                        self.remote(5 + h, q, ref if src is None else src, ref, {"dp": me + (h + 1) * C}).start()
+
+                    @pl.when(z > h)
+                    def _(h=h):
+                        self.remote(8 + h, q, ref if src is None else src, ref, {"dp": me - (h + 1) * C}).start()
+
+            placed(q, act)
+
+        def straight_wait(self, q):
+            for h in range(Z - 1):
+                self.spread_wait(q, h)
+
+        def straight_sent(self, q):
+            def act(o):
+                ref = self.row(o, q, z)
+                for h in range(Z - 1):
+
+                    @pl.when(z + h + 1 < Z)
+                    def _(h=h):
+                        self.remote(5 + h, q, ref, ref, {"dp": me + (h + 1) * C}).wait_send()
+
+                    @pl.when(z > h)
+                    def _(h=h):
+                        self.remote(8 + h, q, ref, ref, {"dp": me - (h + 1) * C}).wait_send()
+
+            placed(q, act)
+
         def share(self, q):
             def act(o):
                 ref = o.at[:, :, c, self.at(q)]
@@ -302,7 +338,14 @@
             slot = lax.rem(q, RING)
             total = f(self.own.at[slot, y, z]) + f(self.part.at[slot, y, z]) + f(self.ry.at[slot, z])
             self.step(q, total + f(self.rl.at[slot, z]) + f(self.rr.at[slot, z]))
-            self.spread(q, 0, self.nw.at[lax.rem(q, SENDS)])
+
+            @pl.when(q < n - SHORT)
+            def _():
+                self.spread(q, 0, self.nw.at[lax.rem(q, SENDS)])
+
+            @pl.when(q >= n - SHORT)
+            def _():
+                self.straight(q, self.nw.at[lax.rem(q, SENDS)])
 
         def y_spread(self, q):
             def act(o):
@@ -382,13 +425,15 @@
         return [pltpu.make_async_copy(src, dst, ahead_sem.at[i]) for i, (src, dst) in enumerate(pairs)]
 
     def iteration(t, _):
-        def at(stage, *acts):
+        def at(stage, *acts, first=0, end=n):
             q = t - stage
 
-            @pl.when((q >= 0) & (q < n))
+            @pl.when((q >= first) & (q < end))
             def _():
                 for act in acts:
                     act(q)
+
+        long, short = {"end": n - SHORT}, {"first": n - SHORT}
 
         def hop(act, h):
             return lambda q: act(q, h)
@@ -399,31 +444,38 @@
         at(2 + DRAIN, hop(a.z_sent, 1), hop(b.z_sent, 2))
         at(3 + DRAIN, hop(a.z_sent, 2), hop(b.z_sent, 3))
         at(4 + DRAIN, hop(a.z_sent, 3), b.y_sent)
-        at(5 + DRAIN, hop(a.spread_sent, 0), b.y_spread_sent)
-        at(6 + DRAIN, hop(a.spread_sent, 1), hop(b.spread_sent, 0))
-        at(7 + DRAIN, hop(a.spread_sent, 2), hop(b.spread_sent, 1))
-        at(8 + DRAIN, a.y_spread_sent, hop(b.spread_sent, 2))
-        at(9 + DRAIN, a.share_sent, b.share_sent)
+        at(5 + DRAIN, b.y_spread_sent)
+        at(5 + DRAIN, hop(a.spread_sent, 0), **long)
+        at(6 + DRAIN, hop(a.spread_sent, 1), hop(b.spread_sent, 0), **long)
+        at(7 + DRAIN, hop(a.spread_sent, 2), hop(b.spread_sent, 1), **long)
+        at(8 + DRAIN, a.y_spread_sent, hop(b.spread_sent, 2), **long)
+        at(9 + DRAIN, a.share_sent, b.share_sent, **long)
         at(3, a.state, b.state)
         at(1, a.terms_wait, a.y_send)
-        at(8, hop(a.spread_wait, 2), a.y_spread)
-        at(7, hop(a.spread_wait, 1), hop(a.spread, 2))
-        at(6, a.weight_stored, hop(a.spread_wait, 0), hop(a.spread, 1))
+        at(8, hop(a.spread_wait, 2), a.y_spread, **long)
+        at(7, hop(a.spread_wait, 1), hop(a.spread, 2), **long)
+        at(6, a.weight_stored, hop(a.spread_wait, 0), hop(a.spread, 1), **long)
+        at(6, a.weight_stored, a.straight_wait, a.y_spread, **short)
         at(2, a.y_wait, hop(a.z_send, 1))
         at(3, hop(a.z_wait, 1), hop(a.z_send, 2))
         at(4, hop(a.z_wait, 2), hop(a.z_send, 3))
         at(5, hop(a.z_wait, 3), a.finish)
-        at(9, a.y_spread_wait, a.share)
+        at(9, a.y_spread_wait, a.share, **long)
+        at(7, a.y_spread_wait, a.share, **short)
         at(1, b.terms_wait, hop(b.z_send, 1))
-        at(8, hop(b.spread_wait, 1), hop(b.spread, 2))
-        at(7, hop(b.spread_wait, 0), hop(b.spread, 1))
-        at(6, b.weight_stored, b.y_spread_wait, hop(b.spread, 0))
+        at(8, hop(b.spread_wait, 1), hop(b.spread, 2), **long)
+        at(7, hop(b.spread_wait, 0), hop(b.spread, 1), **long)
+        at(6, b.weight_stored, b.y_spread_wait, hop(b.spread, 0), **long)
+        at(6, b.weight_stored, b.y_spread_wait, b.straight, **short)
         at(2, hop(b.z_wait, 1), hop(b.z_send, 2))
         at(3, hop(b.z_wait, 2), hop(b.z_send, 3))
         at(4, hop(b.z_wait, 3), b.y_send)
         at(5, b.y_wait, b.finish)
-        at(9, hop(b.spread_wait, 2), b.share)
-        at(10, a.share_wait, b.share_wait)
+        at(9, hop(b.spread_wait, 2), b.share, **long)
+        at(7, b.straight_wait, b.share, **short)
+        at(10, a.share_wait, b.share_wait, **long)
+        at(8, a.share_wait, b.share_wait, **short)
+        at(9, a.straight_sent, b.straight_sent, a.y_spread_sent, a.share_sent, b.share_sent, **short)
 
         @pl.when(t == n + 5)
         def _():
@@ -534,8 +586,8 @@
                 *buffers(small, (Y,)),
                 *held,
                 pltpu.SemaphoreType.DMA((10, SENDS)),
-                pltpu.SemaphoreType.DMA((24, SENDS)),
-                pltpu.SemaphoreType.DMA((24, SENDS)),
+                pltpu.SemaphoreType.DMA((24, SEMS)),
+                pltpu.SemaphoreType.DMA((24, SEMS)),
                 pltpu.SemaphoreType.DMA((1 + 2 * split,)),
             ],
             compiler_params=pltpu.CompilerParams(collective_id=0, has_side_effects=True, vmem_limit_bytes=limit),

time: 539 us -> 539 us (level)
  no operation moved by 1% of the time
where the time goes in v4:
time: 539 us; the launch traced here: 538 us
  Pallas kernels  538 us (100%)
    pallas_call x1, Pallas kernels, step(): pl.pallas_call(functools.partial(kernel, split, tiles), out_shape=(pltpu....  505 us
    pallas_call x1, Pallas kernels, step(): pl.pallas_call(functools.partial(store, split, tiles), out_shape=[jax.Sha...  33.1 us

profile of v4, /device:TPU:0, one launch (start us, length us, event | category | flops | bytes accessed | tf_op | source)
XLA Modules:
  0.0 538.4 jit_solution(4956807119508252072)
XLA Ops:
  0.6 504.6 %step.1 = (bf16[3,2,4,2,320,8,128]{6,5,4,3,2,1,0:T(8,128)(2,1)}, bf16[3,2,4,2,320,8,128]{6,5,4,3,2,1,0:T(8,128)(2,1)S(1)}, f32[2,6,320,8,128]{4,3,2,1,0:T(8,128)...) custom-call(bf16[2,2,4,2,320,8,128]{6,5,4,3,2,1,0:T(8,128)(2,1)} %bi, ...), custom_call_target="tpu_custom_call" | custom-call | tf_op jit(solution)/shard_map/step/pallas_call | solution.py:573
  505.3 33.1 %store.1 = (bf16[2,2,4,2,320,8,128]{6,5,4,3,2,1,0:T(8,128)(2,1)}, bf16[2,2,4,2,320,8,128]{6,5,4,3,2,1,0:T(8,128)(2,1)}, bf16[2,2,4,2,320,8,128]{6,5,4,3,2,1,0:T(...) custom-call(bf16[3,2,4,2,320,8,128]{6,5,4,3,2,1,0:T(8,128)(2,1)} %ge, ...), custom_call_target="tpu_custom_call" | custom-call | tf_op jit(solution)/shard_map/store/pallas_call | solution.py:597
